TPU v7x, 32 devices: a whole 2x2x4 slice. The times are simulated.
32 devices in a mesh: prompt: 4 (over y, core), span: 8 (over z, x).
Axes of the slice: x: 2, y: 2, z: 4, core: 2. Of those that a mesh axis runs over, the one named last changes fastest.
Arguments:
- queries: bfloat16 [32, 8, 8192], P('prompt', 'span'), may hold values from -40 to 40
- query_pos: int32 [32, 8], P('prompt', 'span'), may hold values from 2 to 4095
- fresh_keys: bfloat16 [32, 8, 1024], P('prompt', 'span'), may hold values from -20 to 20
- fresh_values: bfloat16 [32, 8, 1024], P('prompt', 'span'), may hold values from -6 to 6
- cache_keys: bfloat16 [4, 8, 512, 1024], P('prompt', 'span'), may hold values from -18 to 18
- cache_values: bfloat16 [4, 8, 512, 1024], P('prompt', 'span'), may hold values from -6 to 6
- block_len: int32 [4, 8], P('prompt', 'span'), may hold values from 128 to 512
- block_owner: int32 [8, 32, 1], P('span', 'prompt'), may hold values from 0 to 3; in each aligned block of 8 rows (0 to 7, 8 to 15, ..., all dimensions but the last counted through in order) at most 4 rows name the same one
Outputs:
- attended: bfloat16 [32, 8, 8192], P('prompt', 'span')
Inputs may be any that keep to these rules, and one draw needn't show every extreme that they name: `block_owner`: among the 8 prompts of one device, at most 4 name the same stored passage for one passage position.
All inputs are finite; a program needn't handle non-finite values.
Results may differ from a plain program's by a relative error of at most 0.01.
Values may be sent and summed in bfloat16 or wider, within the bound.
A program may use at most 128 MiB of HBM per device.

v0:
```python
import math

import jax
import jax.numpy as jnp
from jax import lax
from jax.sharding import PartitionSpec as P

H = 64
KVH = 8
HD = 128


NEGATIVE = -1e30


def attend(q_rows, pos_rows, key_rows, values, length, col_start):
    row_count = q_rows.shape[0]
    group_size = H // KVH
    slot_ids = lax.broadcasted_iota(jnp.int32, (1, key_rows.shape[0]), 1)
    usable = (slot_ids < length) & (col_start + slot_ids < pos_rows[:, None])

    def per_head(head_id):
        q_part = lax.dynamic_slice_in_dim(q_rows, head_id * group_size * HD, group_size * HD, 1)
        q_part = q_part.reshape(row_count * group_size, HD)
        k_part = lax.dynamic_slice_in_dim(key_rows, head_id * HD, HD, 1)
        v_part = lax.dynamic_slice_in_dim(values, head_id * HD, HD, 1)
        scores = lax.dot_general(
            q_part, k_part, (((1,), (1,)), ((), ())), preferred_element_type=jnp.float32
        )
        scores = scores.reshape(row_count, group_size, -1) / math.sqrt(HD)
        visible = usable[:, None, :]
        maxima = jnp.max(jnp.where(visible, scores, NEGATIVE), axis=2).astype(jnp.bfloat16)
        weights = jnp.where(visible, jnp.exp(scores - maxima.astype(jnp.float32)[:, :, None]), 0.0)
        totals = jnp.sum(weights, axis=2).astype(jnp.bfloat16)
        mixture = jnp.dot(
            weights.astype(jnp.bfloat16).reshape(row_count * group_size, -1),
            v_part,
            preferred_element_type=jnp.float32,
        )
        return (mixture.astype(jnp.bfloat16).reshape(row_count, group_size * HD), maxima, totals)

    mixture, maxima, totals = lax.map(per_head, jnp.arange(KVH, dtype=jnp.int32))
    mixture = jnp.transpose(mixture, (1, 0, 2)).reshape(row_count, H * HD)
    maxima = jnp.transpose(maxima, (1, 0, 2)).reshape(row_count, H)
    totals = jnp.transpose(totals, (1, 0, 2)).reshape(row_count, H)
    return (mixture, maxima, totals)


def on_device(
    queries, query_pos, fresh_keys, fresh_values, cache_keys, cache_values, block_len, block_owner
):
    prompts = queries.shape[0]
    own_rows = queries.shape[1]
    group_size = H // KVH
    column = lax.axis_index("span")
    row_owners = lax.axis_size("prompt")
    col_start = column * cache_keys.shape[2]
    gathered_q, gathered_pos = (
        lax.all_gather(queries, "span", axis=1, tiled=True),
        lax.all_gather(query_pos, "span", axis=1, tiled=True),
    )
    selected = gathered_q.shape[1]
    targets = block_owner[0, :, 0]
    capacity = max(2, 2 * prompts // row_owners)
    earlier = lax.broadcasted_iota(jnp.int32, (prompts, prompts), 1) < lax.broadcasted_iota(
        jnp.int32, (prompts, prompts), 0
    )
    same_row = targets[None, :] == targets[:, None]
    slot_rank = jnp.sum((same_row & earlier).astype(jnp.int32), axis=1)
    slot_place = targets * capacity + slot_rank
    slot_ids = lax.broadcasted_iota(jnp.int32, (row_owners * capacity, prompts), 0)
    one_hot = slot_ids == slot_place[None, :]
    send_q = jnp.dot(
        one_hot.astype(jnp.bfloat16),
        gathered_q.reshape(prompts, -1),
        preferred_element_type=jnp.float32,
    ).astype(jnp.bfloat16)
    send_q = send_q.reshape(row_owners, capacity, selected, H * HD)
    send_pos = jnp.sum(jnp.where(one_hot[:, :, None], gathered_pos[None], 0), axis=1)
    send_pos = send_pos.reshape(row_owners, capacity, selected)
    local_keys = cache_keys[0, 0]
    local_values = cache_values[0, 0]
    local_len = block_len[0, 0]
    q_items = lax.all_to_all(send_q, "prompt", split_axis=0, concat_axis=0, tiled=True)
    pos_items = lax.all_to_all(send_pos, "prompt", split_axis=0, concat_axis=0, tiled=True)
    item_shape = q_items.shape
    mixture, maxima, totals = attend(
        q_items.reshape(-1, item_shape[-1]),
        pos_items.reshape(-1),
        local_keys,
        local_values,
        local_len,
        col_start,
    )
    stat_shape = item_shape[:-1] + (H,)
    answered = (mixture.reshape(item_shape), maxima.reshape(stat_shape), totals.reshape(stat_shape))
    back_mix, back_max, back_tot = answered
    back_mix, back_max, back_tot = (
        lax.all_to_all(back_mix, "prompt", split_axis=0, concat_axis=0, tiled=True),
        lax.all_to_all(back_max, "prompt", split_axis=0, concat_axis=0, tiled=True),
        lax.all_to_all(back_tot, "prompt", split_axis=0, concat_axis=0, tiled=True),
    )
    pick_back = jnp.transpose(one_hot)
    part_mix = jnp.dot(
        pick_back.astype(jnp.bfloat16),
        back_mix.reshape(row_owners * capacity, -1),
        preferred_element_type=jnp.float32,
    ).astype(jnp.bfloat16)
    part_mix = part_mix.reshape(prompts, selected, H * HD)
    pick_float = pick_back.astype(jnp.float32)
    part_max = (
        jnp.einsum(
            "ps,sr->pr",
            pick_float,
            back_max.reshape(row_owners * capacity, -1).astype(jnp.float32),
            precision=lax.Precision.HIGHEST,
        )
        .astype(jnp.bfloat16)
        .reshape(prompts, selected, H)
    )
    part_tot = (
        jnp.einsum(
            "ps,sr->pr",
            pick_float,
            back_tot.reshape(row_owners * capacity, -1).astype(jnp.float32),
            precision=lax.Precision.HIGHEST,
        )
        .astype(jnp.bfloat16)
        .reshape(prompts, selected, H)
    )
    own_q = queries.reshape(prompts, own_rows, KVH, group_size, HD)
    own_k = fresh_keys.reshape(prompts, own_rows, KVH, HD)
    own_score = jnp.einsum("psgxd,psgd->psgx", own_q, own_k, preferred_element_type=jnp.float32)
    own_score = own_score.reshape(prompts, own_rows, H) / math.sqrt(HD)
    own_value = jnp.broadcast_to(
        fresh_values.astype(jnp.float32).reshape(prompts, own_rows, KVH, 1, HD),
        (prompts, own_rows, KVH, group_size, HD),
    ).reshape(prompts, own_rows, H, HD)
    recv_mix, recv_max, recv_tot = (
        lax.all_to_all(part_mix[None], "span", split_axis=2, concat_axis=0, tiled=True),
        lax.all_to_all(part_max[None], "span", split_axis=2, concat_axis=0, tiled=True),
        lax.all_to_all(part_tot[None], "span", split_axis=2, concat_axis=0, tiled=True),
    )
    recv_float = recv_max.astype(jnp.float32)
    top_own = jnp.max(recv_float, axis=0)
    factor = jnp.exp(recv_float - top_own[None])
    summed_mix = jnp.sum(
        recv_mix.astype(jnp.float32).reshape(recv_mix.shape[0], prompts, own_rows, H, HD)
        * factor[..., None],
        axis=0,
    ).reshape(prompts, own_rows, H * HD)
    summed_tot = jnp.sum(recv_tot.astype(jnp.float32) * factor, axis=0)
    highest = jnp.maximum(top_own, own_score)
    keep_scale = jnp.exp(top_own - highest)
    fresh_scale = jnp.exp(own_score - highest)
    numer = (
        keep_scale[..., None] * summed_mix.reshape(prompts, own_rows, H, HD)
        + fresh_scale[..., None] * own_value
    )
    denom = keep_scale * summed_tot + fresh_scale
    return (numer / denom[..., None]).reshape(prompts, own_rows, H * HD).astype(jnp.bfloat16)


def solution(mesh):
    return jax.shard_map(
        on_device,
        mesh=mesh,
        in_specs=(
            P("prompt", "span", None),
            P("prompt", "span"),
            P("prompt", "span", None),
            P("prompt", "span", None),
            P("prompt", "span", None, None),
            P("prompt", "span", None, None),
            P("prompt", "span"),
            P("span", "prompt", None),
        ),
        out_specs=P("prompt", "span", None),
        check_vma=False,
    )
```

profile of v0, /device:TPU:0, one launch (start us, length us, event | category | flops | bytes accessed | tf_op | source)
XLA Modules:
  0.0 244.3 jit_solution(4959912699700051304)
XLA Ops:
  6.5 0.7 all-gather.3.cloned.1.call-update
  7.3 22.4 %all-gather = s32[8,1,8]{2,1,0:T(1,128)S(1)} all-gather(s32[1,1,8]{2,1,0:T(1,128)} %bitcast.164), channel_id=1, replica_groups=mesh['prompt'=4,'span'=8] {'span'}, dimensions={0}, use_global_device_ids=true | all-gather | bytes 288 | tf_op jit(solution)/shard_map/all_gather | solution.py:60
  29.8 0.9 convert_reduce_fusion
  31.5 0.7 copy.54
  32.2 3.2 %all-to-all-start = ((s32[4,4,8]{2,1,0:T(4,128)}), s32[4,4,8]{2,1,0:T(4,128)S(1)}, u32[]{:S(2)}, u32[]{:S(2)}) async-start(s32[4,4,8]{2,1,0:T(4,128)} %bitcast.8), calls=%async_computation | async-start | bytes 16384 | tf_op jit(solution)/shard_map/all_to_all | solution.py:85
  35.4 17.0 %all-gather.3.cloned.1.call-done = bf16[8,8,8192]{2,0,1:T(8,128)(2,1)} async-done(((bf16[8,1,8192]{2,0,1:T(8,128)(2,1)}), bf16[8,8,8192]{2,0,1:T(8,128)(2,1)}) %all-gather.3.cloned.1.call-update) | async-done | bytes 1048592 | tf_op jit(solution)/shard_map/all_gather | solution.py:59
  52.5 2.0 convolution_convert_fusion.1
  54.5 2.5 %copy.72 = bf16[2,8,8,8192]{3,2,1,0:T(8,128)(2,1)} copy(bf16[2,8,8,8192]{3,1,2,0:T(8,128)(2,1)S(1)} %bitcast.151) | data formatting | bytes 4194304
  57.0 3.6 %all-to-all-start.1 = ((bf16[4,4,8,8192]{3,2,1,0:T(8,128)(2,1)}), bf16[4,4,8,8192]{3,2,1,0:T(8,128)(2,1)S(1)}, u32[]{:S(2)}, u32[]{:S(2)}) async-start(bf16[4,4,8,8192]{3,2,1,0:T(8,128)(2,1)} %bitcast.55), calls=%async_computation.1 | async-start | bytes 4194304 | tf_op jit(solution)/shard_map/all_to_all | solution.py:84
  61.4 24.8 %all-to-all-done.1 = bf16[4,4,8,8192]{3,2,1,0:T(8,128)(2,1)S(1)} async-done(((bf16[4,4,8,8192]{3,2,1,0:T(8,128)(2,1)}), bf16[4,4,8,8192]{3,2,1,0:T(8,128)(2,1)S(1)}, u32[]{:S(2)}, u32[]{:S(2)}) %all-to-all-start.1) | async-done | bytes 2097184 | tf_op jit(solution)/shard_map/all_to_all | solution.py:84
  86.2 56.6 %while.17 = (s32[]{:T(128)}, bf16[8,128,1024]{2,1,0:T(8,128)(2,1)}, bf16[8,128,8]{1,2,0:T(8,128)(2,1)S(1)}, bf16[8,128,8]{1,2,0:T(8,128)(2,1)S(1)}, s32[8]{0:T(1...) while((s32[]{:T(128)}, bf16[8,128,1024]{2,1,0:T(8,128)(2,1)}, ...), condition=%wide.region_5.6_spmd.clone, body=%wide.region_2.5_spmd.clone.sunk | while | flops 272890880 | bytes 9398037 | solution.py:42
  88.6 1.5 select_reduce_fusion.3
  90.1 0.7 fusion.46
  90.8 1.6 convolution_convert_fusion.6
  92.6 0.7 constant_dynamic-update-slice_fusion.2
  95.6 1.5 select_reduce_fusion.3
  97.1 0.7 fusion.46
  97.9 1.6 convolution_convert_fusion.6
  99.6 0.7 constant_dynamic-update-slice_fusion.2
  102.7 1.5 select_reduce_fusion.3
  104.2 0.7 fusion.46
  104.9 1.6 convolution_convert_fusion.6
  106.7 0.7 constant_dynamic-update-slice_fusion.2
  109.8 1.5 select_reduce_fusion.3
  111.3 0.7 fusion.46
  112.0 1.6 convolution_convert_fusion.6
  113.8 0.7 constant_dynamic-update-slice_fusion.2
  116.8 1.5 select_reduce_fusion.3
  118.3 0.7 fusion.46
  119.1 1.6 convolution_convert_fusion.6
  120.8 0.7 constant_dynamic-update-slice_fusion.2
  123.9 1.5 select_reduce_fusion.3
  125.4 0.7 fusion.46
  126.1 1.6 convolution_convert_fusion.6
  127.9 0.7 constant_dynamic-update-slice_fusion.2
  131.0 1.5 select_reduce_fusion.3
  132.5 0.7 fusion.46
  133.2 1.6 convolution_convert_fusion.6
  135.0 0.7 constant_dynamic-update-slice_fusion.2
  138.1 1.5 select_reduce_fusion.3
  139.5 0.7 fusion.46
  140.3 1.6 convolution_convert_fusion.6
  142.0 0.7 constant_dynamic-update-slice_fusion.2
  143.4 0.7 reshape.346
  144.1 3.3 %all-to-all-start.2 = ((bf16[4,2,1024]{2,1,0:T(2,128)(2,1)}), bf16[4,2,1024]{2,1,0:T(2,128)(2,1)S(1)}, u32[]{:S(2)}, u32[]{:S(2)}) async-start(bf16[4,2,1024]{2,1,0:T(2,128)(2,1)} %reshape.346), calls=%async_computation.2 | async-start | bytes 32768 | tf_op jit(solution)/shard_map/all_to_all | solution.py:100
  147.9 0.7 reshape.350
  148.6 2.5 %all-to-all-done.2 = bf16[4,2,1024]{2,1,0:T(2,128)(2,1)S(1)} async-done(((bf16[4,2,1024]{2,1,0:T(2,128)(2,1)}), bf16[4,2,1024]{2,1,0:T(2,128)(2,1)S(1)}, u32[]{:S(2)}, u32[]{:S(2)}) %all-to-all-start.2) | async-done | bytes 16416 | tf_op jit(solution)/shard_map/all_to_all | solution.py:100
  151.1 3.2 %all-to-all-start.6 = ((bf16[4,2,1024]{2,1,0:T(2,128)(2,1)}), bf16[4,2,1024]{2,1,0:T(2,128)(2,1)S(1)}, u32[]{:S(2)}, u32[]{:S(2)}) async-start(bf16[4,2,1024]{2,1,0:T(2,128)(2,1)} %reshape.350), calls=%async_computation.6 | async-start | bytes 32768 | tf_op jit(solution)/shard_map/all_to_all | solution.py:101
  154.4 2.7 %copy.59 = bf16[128,8,1024]{2,1,0:T(8,128)(2,1)S(1)} copy(bf16[128,8,1024]{2,0,1:T(8,128)(2,1)} %bitcast.153) | data formatting | bytes 4194304 | tf_op jit(solution)/shard_map/transpose | solution.py:43
  157.1 2.4 reshape_reshape.10
  159.5 3.6 %all-to-all-start.4 = ((bf16[4,4,8,8192]{3,2,1,0:T(8,128)(2,1)}), bf16[4,4,8,8192]{3,2,1,0:T(8,128)(2,1)S(1)}, u32[]{:S(2)}, u32[]{:S(2)}) async-start(bf16[4,4,8,8192]{3,2,1,0:T(8,128)(2,1)} %reshape_reshape.10), calls=%async_computation.4 | async-start | bytes 4194304 | tf_op jit(solution)/shard_map/all_to_all | solution.py:99
  163.6 0.7 reshape.348
  164.5 24.3 %all-to-all-done.4 = bf16[4,4,8,8192]{3,2,1,0:T(8,128)(2,1)S(1)} async-done(((bf16[4,4,8,8192]{3,2,1,0:T(8,128)(2,1)}), bf16[4,4,8,8192]{3,2,1,0:T(8,128)(2,1)S(1)}, u32[]{:S(2)}, u32[]{:S(2)}) %all-to-all-start.4) | async-done | bytes 2097184 | tf_op jit(solution)/shard_map/all_to_all | solution.py:99
  188.7 3.3 %all-to-all-start.3 = ((bf16[8,2,256]{2,1,0:T(2,128)(2,1)}), bf16[8,2,256]{2,1,0:T(2,128)(2,1)S(1)}, u32[]{:S(2)}, u32[]{:S(2)}) async-start(bf16[8,2,256]{2,1,0:T(2,128)(2,1)} %reshape.348), calls=%async_computation.3 | async-start | bytes 16384 | tf_op jit(solution)/shard_map/all_to_all | solution.py:141
  192.4 0.7 reshape.352
  193.1 2.5 %copy.73 = bf16[2,8,8,8192]{3,1,2,0:T(8,128)(2,1)} copy(bf16[2,8,8,8192]{3,2,1,0:T(8,128)(2,1)S(1)} %bitcast.149) | data formatting | bytes 4194304
  195.6 3.0 %all-to-all-done.3 = bf16[8,2,256]{2,1,0:T(2,128)(2,1)S(1)} async-done(((bf16[8,2,256]{2,1,0:T(2,128)(2,1)}), bf16[8,2,256]{2,1,0:T(2,128)(2,1)S(1)}, u32[]{:S(2)}, u32[]{:S(2)}) %all-to-all-start.3) | async-done | bytes 8224 | tf_op jit(solution)/shard_map/all_to_all | solution.py:141
  198.6 3.3 %all-to-all-start.7 = ((bf16[8,2,256]{2,1,0:T(2,128)(2,1)}), bf16[8,2,256]{2,1,0:T(2,128)(2,1)S(1)}, u32[]{:S(2)}, u32[]{:S(2)}) async-start(bf16[8,2,256]{2,1,0:T(2,128)(2,1)} %reshape.352), calls=%async_computation.7 | async-start | bytes 16384 | tf_op jit(solution)/shard_map/all_to_all | solution.py:142
  201.9 3.1 %convolution_convert_fusion.2 = bf16[8,65536]{1,0:T(8,128)(2,1)} fusion(bf16[16,65536]{1,0:T(8,128)(2,1)} %bitcast.150, s32[8]{0:T(128)S(1)} %multiply_add_fusion.1), kind=kOutput, calls=%fused_computation.21 | convolution fusion | flops 17301632 | bytes 3145760 | tf_op jit(solution)/shard_map/dot_general | solution.py:104
  205.0 3.3 %all-to-all-done.7 = bf16[8,2,256]{2,1,0:T(2,128)(2,1)S(1)} async-done(((bf16[8,2,256]{2,1,0:T(2,128)(2,1)}), bf16[8,2,256]{2,1,0:T(2,128)(2,1)S(1)}, u32[]{:S(2)}, u32[]{:S(2)}) %all-to-all-start.7) | async-done | bytes 8224 | tf_op jit(solution)/shard_map/all_to_all | solution.py:142
  208.4 3.6 %all-to-all-start.5 = ((bf16[1,8,8,8192]{3,1,0,2:T(8,128)(2,1)}), bf16[1,8,8,8192]{3,1,0,2:T(8,128)(2,1)S(1)}, u32[]{:S(2)}, u32[]{:S(2)}) async-start(bf16[1,8,8,8192]{3,1,0,2:T(8,128)(2,1)} %bitcast.21), calls=%async_computation.5 | async-start | bytes 2097152 | tf_op jit(solution)/shard_map/all_to_all | solution.py:140
  212.9 22.8 %all-to-all-done.5 = bf16[1,8,8,8192]{3,1,0,2:T(8,128)(2,1)S(1)} async-done(((bf16[1,8,8,8192]{3,1,0,2:T(8,128)(2,1)}), bf16[1,8,8,8192]{3,1,0,2:T(8,128)(2,1)S(1)}, u32[]{:S(2)}, u32[]{:S(2)}) %all-to-all-start.5) | async-done | bytes 1048608 | tf_op jit(solution)/shard_map/all_to_all | solution.py:140
  235.7 0.7 fusion.13
  236.5 0.9 fusion.14
  (106 shorter events, 12.8 us)
Async XLA Ops:
  6.5 205.4 %copy-start = (bf16[8,1,1024]{2,0,1:T(8,128)(2,1)S(1)}, bf16[8,1,1024]{2,0,1:T(8,128)(2,1)}, u32[]{:S(2)}) copy-start(bf16[8,1,1024]{2,0,1:T(8,128)(2,1)} %param.12) | copy-start | bytes 49156
  6.5 45.9 %all-gather.3.cloned.1.call-start = ((), (), s32[]{:S(2)}) async-start(), calls=%async_computation.8 | async-start | bytes 1179648 | tf_op jit(solution)/shard_map/all_gather | solution.py:59
  32.2 24.8 %all-to-all-start = ((s32[4,4,8]{2,1,0:T(4,128)}), s32[4,4,8]{2,1,0:T(4,128)S(1)}, u32[]{:S(2)}, u32[]{:S(2)}) async-start(s32[4,4,8]{2,1,0:T(4,128)} %bitcast.8), calls=%async_computation | async-start | bytes 16384 | tf_op jit(solution)/shard_map/all_to_all | solution.py:85
  57.0 29.2 %all-to-all-start.1 = ((bf16[4,4,8,8192]{3,2,1,0:T(8,128)(2,1)}), bf16[4,4,8,8192]{3,2,1,0:T(8,128)(2,1)S(1)}, u32[]{:S(2)}, u32[]{:S(2)}) async-start(bf16[4,4,8,8192]{3,2,1,0:T(8,128)(2,1)} %bitcast.55), calls=%async_computation.1 | async-start | bytes 4194304 | tf_op jit(solution)/shard_map/all_to_all | solution.py:84
  144.1 7.1 %all-to-all-start.2 = ((bf16[4,2,1024]{2,1,0:T(2,128)(2,1)}), bf16[4,2,1024]{2,1,0:T(2,128)(2,1)S(1)}, u32[]{:S(2)}, u32[]{:S(2)}) async-start(bf16[4,2,1024]{2,1,0:T(2,128)(2,1)} %reshape.346), calls=%async_computation.2 | async-start | bytes 32768 | tf_op jit(solution)/shard_map/all_to_all | solution.py:100
  151.1 8.3 %all-to-all-start.6 = ((bf16[4,2,1024]{2,1,0:T(2,128)(2,1)}), bf16[4,2,1024]{2,1,0:T(2,128)(2,1)S(1)}, u32[]{:S(2)}, u32[]{:S(2)}) async-start(bf16[4,2,1024]{2,1,0:T(2,128)(2,1)} %reshape.350), calls=%async_computation.6 | async-start | bytes 32768 | tf_op jit(solution)/shard_map/all_to_all | solution.py:101
  159.5 29.2 %all-to-all-start.4 = ((bf16[4,4,8,8192]{3,2,1,0:T(8,128)(2,1)}), bf16[4,4,8,8192]{3,2,1,0:T(8,128)(2,1)S(1)}, u32[]{:S(2)}, u32[]{:S(2)}) async-start(bf16[4,4,8,8192]{3,2,1,0:T(8,128)(2,1)} %reshape_reshape.10), calls=%async_computation.4 | async-start | bytes 4194304 | tf_op jit(solution)/shard_map/all_to_all | solution.py:99
  188.7 9.8 %all-to-all-start.3 = ((bf16[8,2,256]{2,1,0:T(2,128)(2,1)}), bf16[8,2,256]{2,1,0:T(2,128)(2,1)S(1)}, u32[]{:S(2)}, u32[]{:S(2)}) async-start(bf16[8,2,256]{2,1,0:T(2,128)(2,1)} %reshape.348), calls=%async_computation.3 | async-start | bytes 16384 | tf_op jit(solution)/shard_map/all_to_all | solution.py:141
  198.6 9.8 %all-to-all-start.7 = ((bf16[8,2,256]{2,1,0:T(2,128)(2,1)}), bf16[8,2,256]{2,1,0:T(2,128)(2,1)S(1)}, u32[]{:S(2)}, u32[]{:S(2)}) async-start(bf16[8,2,256]{2,1,0:T(2,128)(2,1)} %reshape.352), calls=%async_computation.7 | async-start | bytes 16384 | tf_op jit(solution)/shard_map/all_to_all | solution.py:142
  201.9 10.0 %copy-start.1 = (bf16[8,1,8192]{2,0,1:T(8,128)(2,1)S(1)}, bf16[8,1,8192]{2,0,1:T(8,128)(2,1)}, u32[]{:S(2)}) copy-start(bf16[8,1,8192]{2,0,1:T(8,128)(2,1)} %param.10) | copy-start | bytes 393220
  201.9 10.3 %copy-start.2 = (bf16[8,1,1024]{2,0,1:T(8,128)(2,1)S(1)}, bf16[8,1,1024]{2,0,1:T(8,128)(2,1)}, u32[]{:S(2)}) copy-start(bf16[8,1,1024]{2,0,1:T(8,128)(2,1)} %param.13) | copy-start | bytes 49156
  208.4 27.4 %all-to-all-start.5 = ((bf16[1,8,8,8192]{3,1,0,2:T(8,128)(2,1)}), bf16[1,8,8,8192]{3,1,0,2:T(8,128)(2,1)S(1)}, u32[]{:S(2)}, u32[]{:S(2)}) async-start(bf16[1,8,8,8192]{3,1,0,2:T(8,128)(2,1)} %bitcast.21), calls=%async_computation.5 | async-start | bytes 2097152 | tf_op jit(solution)/shard_map/all_to_all | solution.py:140
Sparse Core Ops, SparseCore 0:
  9.5 42.9 all-gather.2
where the time goes:
time: 245 us; the launch traced here: 244 us
  waiting for transfers between devices  98.5 us (40%)
  matrix products  30.7 us (13%)
  local copies, waits for them, and re-layouts  29.7 us (12%)
  starting transfers between devices  27.2 us (11%)
  blocking collectives  22.4 us (9%)
  between operations  14.3 us (6%)
  loops' own time  11.4 us (5%)
  other arithmetic  10 us (4%)
    all_to_all x1, waiting for transfers between devices, on_device(): lax.all_to_all(send_q, 'prompt', split_axis=0, concat_axis=0, tiled=True)  24.8 us
    all_to_all x1, waiting for transfers between devices, on_device(): lax.all_to_all(back_mix, 'prompt', split_axis=0, concat_axis=0, tiled=True)  24.3 us
    all_to_all x1, waiting for transfers between devices, on_device(): lax.all_to_all(part_mix[None], 'span', split_axis=2, concat_axis=0, tiled...  22.8 us
    all_gather x1, blocking collectives, on_device(): lax.all_gather(query_pos, 'span', axis=1, tiled=True)  22.4 us
    all_gather x1, waiting for transfers between devices, on_device(): lax.all_gather(queries, 'span', axis=1, tiled=True)  17 us
    dot_general x8, matrix products, per_head(): jnp.dot(weights.astype(jnp.bfloat16).reshape(row_count * group_size, -1),...  13.1 us
    dot_general x8, matrix products, per_head(): lax.dot_general(q_part, k_part, (((1,), (1,)), ((), ())), preferred_eleme...  11.9 us
    another operation x1, loops' own time, attend(): lax.map(per_head, jnp.arange(KVH, dtype=jnp.int32))  11.4 us
  transfers between devices with their start and end apart: 9, of which 7 were waited for; matrix products, arithmetic and copies ran while one was open for 9% of the time, Pallas kernels for 0%

commit v1 on v0

v1 whole, which is shorter than its diff:
```python
import functools
import math

import jax
import jax.numpy as jnp
from jax import lax
from jax.experimental import pallas as pl
from jax.experimental.pallas import tpu as pltpu
from jax.sharding import PartitionSpec as P

H = 64
KVH = 8
HD = 128
XH = H // KVH
NEGATIVE = -1e30
MESH = pl.DeviceIdType.MESH
CORES = 2


def kernel(
    np_, ns, prompts, slots,
    owner_ref, q_ref, pos_ref, fk_ref, fv_ref, k_ref, v_ref, len_ref,
    out_ref,
    q_all, pos_all, len_all, part, part_all, stat, stat_all, own_ref,
    q_send, q_recv, pos_send, pos_recv, len_send, len_recv,
    load_sem, kvy_send, kvy_recv, kvp_send, kvp_recv,
    part_send, part_recv, stat_send, stat_recv, keep_sem, own_sem,
    *kv,
):
    row = lax.axis_index("prompt")
    col = lax.axis_index("span")
    rows_y = np_ // CORES
    core = lax.rem(row, CORES)
    partner = row + 1 - 2 * core

    def wait_bytes(ref, sem):
        pltpu.make_async_copy(ref, ref, sem).wait()

    def send(src, dst, send_sem, recv_sem, p_, s_):
        pltpu.make_async_remote_copy(
            src_ref=src, dst_ref=dst, send_sem=send_sem, recv_sem=recv_sem,
            device_id=(p_, s_), device_id_type=MESH,
        ).start()

    span_peers = [lax.rem(col + d, ns) for d in range(1, ns)]
    row_peers = [lax.rem(row + d, np_) for d in range(1, np_)]
    y_peers = [lax.rem(row + CORES * d, np_) for d in range(1, rows_y)]

    loads = []
    for g in range(KVH):
        cols = pl.ds(g * HD, HD)
        for i, src in enumerate((k_ref, v_ref)):
            c = pltpu.make_async_copy(
                src.at[:, cols], kv[g].at[row, i], load_sem.at[g, i]
            )
            c.start()
            loads.append(c)
    q_keep = pltpu.make_async_copy(q_ref, q_all.at[col], own_sem.at[0])
    q_keep.start()
    pos_keep = pltpu.make_async_copy(pos_ref, pos_all.at[col], own_sem.at[1])
    pos_keep.start()
    len_keep = pltpu.make_async_copy(len_ref, len_all.at[row], own_sem.at[2])
    len_keep.start()

    barrier = pltpu.get_barrier_semaphore()
    for s in span_peers:
        pl.semaphore_signal(barrier, inc=1, device_id=(row, s), device_id_type=MESH)
    for r in row_peers:
        pl.semaphore_signal(barrier, inc=1, device_id=(r, col), device_id_type=MESH)
    pl.semaphore_wait(barrier, ns - 1 + np_ - 1)

    for r in row_peers:
        send(len_ref, len_all.at[row], len_send, len_recv, r, col)
    for s in span_peers:
        send(pos_ref, pos_all.at[col], pos_send, pos_recv, row, s)
    for g in range(KVH):
        loads[2 * g].wait()
        loads[2 * g + 1].wait()
        for r in y_peers:
            send(kv[g].at[row], kv[g].at[row], kvy_send.at[g], kvy_recv.at[g], r, col)
        send(kv[g].at[row], kv[g].at[row], kvp_send.at[g], kvp_recv.at[g], partner, col)
        for s in span_peers:
            send(q_ref.at[g], q_all.at[col, g], q_send.at[g], q_recv.at[g], row, s)

    lane = lax.broadcasted_iota(jnp.int32, (XH, HD), 1)
    own_ref[...] = jnp.zeros_like(own_ref)
    stat[...] = jnp.zeros_like(stat)

    def own_body(p, carry):
        keys = fk_ref[p].astype(jnp.float32)
        tile = own_ref[...]
        for g in range(KVH):
            q8 = q_ref[g, p].astype(jnp.float32)
            dot = jnp.sum(q8 * keys[g : g + 1], axis=1, keepdims=True)
            tile = jnp.where(lane == g * prompts + p, dot * (1.0 / math.sqrt(HD)), tile)
        own_ref[...] = tile
        return carry

    lax.fori_loop(0, prompts, own_body, 0)

    q_keep.wait()
    pos_keep.wait()
    len_keep.wait()
    wait_bytes(len_all.at[pl.ds(0, np_ - 1)], len_recv)
    wait_bytes(pos_all.at[pl.ds(0, ns - 1)], pos_recv)

    count = ns * XH
    slot_ids = lax.broadcasted_iota(jnp.int32, (count, slots), 1)
    lanes3 = lax.broadcasted_iota(jnp.int32, (ns, XH, HD), 2)
    start = col * slots
    step = 2 if prompts % 2 == 0 else 1

    for g in range(KVH):
        wait_bytes(q_all.at[pl.ds(0, ns - 1), g], q_recv.at[g])
        if rows_y > 1:
            wait_bytes(kv[g].at[pl.ds(0, rows_y - 1)], kvy_recv.at[g])
        for r in y_peers:
            send(kv[g].at[r], kv[g].at[r], kvp_send.at[g], kvp_recv.at[g], partner, col)
        wait_bytes(kv[g].at[pl.ds(0, rows_y)], kvp_recv.at[g])

        def one(p, g=g):
            o = owner_ref[p]
            q64 = q_all[:, g, p].astype(jnp.float32).reshape(count, HD).astype(jnp.bfloat16)
            keys = kv[g][o, 0]
            values = kv[g][o, 1]
            pos3 = jnp.broadcast_to(pos_all[:, pl.ds(p, 1), :], (ns, XH, HD))
            len3 = jnp.broadcast_to(len_all[o][None], (ns, XH, HD))
            limit = jnp.minimum(len3, pos3 - start).reshape(count, HD)
            limit = jnp.concatenate([limit] * (slots // HD), axis=1)
            visible = slot_ids < limit
            scores = lax.dot_general(
                q64, keys, (((1,), (1,)), ((), ())), preferred_element_type=jnp.float32
            ) * (1.0 / math.sqrt(HD))
            scores = jnp.where(visible, scores, NEGATIVE)
            top = jnp.max(scores, axis=1, keepdims=True)
            top = top.astype(jnp.bfloat16).astype(jnp.float32)
            weights = jnp.where(visible, jnp.exp(scores - top), 0.0)
            total = jnp.sum(weights, axis=1, keepdims=True)
            mix = jnp.dot(
                weights.astype(jnp.bfloat16), values, preferred_element_type=jnp.float32
            )
            part[:, g, p] = mix.reshape(ns, XH, HD).astype(jnp.bfloat16)
            here = lanes3 == g * prompts + p
            top3 = jnp.broadcast_to(top, (count, HD)).reshape(ns, XH, HD)
            total3 = jnp.broadcast_to(total, (count, HD)).reshape(ns, XH, HD)
            stat[:, 0] = jnp.where(here, top3, stat[:, 0])
            stat[:, 1] = jnp.where(here, total3, stat[:, 1])

        def body(i, carry):
            for k in range(step):
                one(i * step + k)
            return carry

        lax.fori_loop(0, prompts // step, body, 0)
        for s in span_peers:
            send(part.at[s, g], part_all.at[col, g], part_send.at[g], part_recv.at[g], row, s)
        pltpu.make_async_copy(part.at[col, g], part_all.at[col, g], keep_sem.at[g]).start()

    for s in span_peers:
        send(stat.at[s], stat_all.at[col], stat_send, stat_recv, row, s)
    pltpu.make_async_copy(stat.at[col], stat_all.at[col], own_sem.at[3]).start()

    wait_bytes(stat.at[col], own_sem.at[3])
    wait_bytes(stat_all.at[pl.ds(0, ns - 1)], stat_recv)
    tops = [stat_all[j, 0] for j in range(ns)]
    own = own_ref[...]
    high = own
    for t in tops:
        high = jnp.maximum(high, t)
    own_w = jnp.exp(own - high)
    factors = [jnp.exp(t - high) for t in tops]
    denom = own_w
    for j in range(ns):
        denom = denom + factors[j] * stat_all[j, 1]
    inv = 1.0 / denom
    for j in range(ns):
        stat_all[j, 0] = factors[j] * inv
    own_ref[...] = own_w * inv

    for g in range(KVH):
        wait_bytes(part.at[col, g], keep_sem.at[g])
        wait_bytes(part_all.at[pl.ds(0, ns - 1), g], part_recv.at[g])

    def combine(p, carry):
        shift = lax.rem(HD - p, HD)
        own_s = pltpu.roll(own_ref[...], shift, 1)
        fresh = fv_ref[p].astype(jnp.float32)
        sums = []
        for g in range(KVH):
            lo = g * prompts
            sums.append(own_s[:, lo : lo + 1] * fresh[g : g + 1])
        for j in range(ns):
            f = pltpu.roll(stat_all[j, 0], shift, 1)
            for g in range(KVH):
                lo = g * prompts
                sums[g] = sums[g] + f[:, lo : lo + 1] * part_all[j, g, p].astype(jnp.float32)
        for g in range(KVH):
            out_ref[p, g] = sums[g].astype(jnp.bfloat16)
        return carry

    lax.fori_loop(0, prompts, combine, 0)

    wait_bytes(len_all.at[pl.ds(0, np_ - 1)], len_send)
    wait_bytes(pos_all.at[pl.ds(0, ns - 1)], pos_send)
    wait_bytes(stat_all.at[pl.ds(0, ns - 1)], stat_send)
    for g in range(KVH):
        wait_bytes(q_all.at[pl.ds(0, ns - 1), g], q_send.at[g])
        if rows_y > 1:
            wait_bytes(kv[g].at[pl.ds(0, rows_y - 1)], kvy_send.at[g])
        wait_bytes(kv[g].at[pl.ds(0, rows_y)], kvp_send.at[g])
        wait_bytes(part_all.at[pl.ds(0, ns - 1), g], part_send.at[g])


def on_device(
    queries, query_pos, fresh_keys, fresh_values, cache_keys, cache_values, block_len, block_owner
):
    prompts = queries.shape[0]
    slots = cache_keys.shape[2]
    np_ = lax.axis_size("prompt")
    ns = lax.axis_size("span")
    q = jnp.transpose(queries.reshape(prompts, KVH, XH, HD), (1, 0, 2, 3))
    pos = jnp.broadcast_to(query_pos.reshape(prompts, 1), (prompts, HD))
    lens = jnp.broadcast_to(block_len.reshape(1, 1), (XH, HD))
    owner = block_owner.reshape(prompts)
    vmem = pl.BlockSpec(memory_space=pltpu.VMEM)
    hbm = pl.BlockSpec(memory_space=pl.ANY)
    dma = pltpu.SemaphoreType.DMA
    bf16, f32, i32 = jnp.bfloat16, jnp.float32, jnp.int32
    out = pl.pallas_call(
        functools.partial(kernel, np_, ns, prompts, slots),
        out_shape=jax.ShapeDtypeStruct((prompts, KVH, XH, HD), bf16),
        in_specs=[pl.BlockSpec(memory_space=pltpu.SMEM)] + [vmem] * 4 + [hbm] * 2 + [vmem],
        out_specs=vmem,
        scratch_shapes=[
            pltpu.VMEM((ns, KVH, prompts, XH, HD), bf16),
            pltpu.VMEM((ns, prompts, HD), i32),
            pltpu.VMEM((np_, XH, HD), i32),
            pltpu.VMEM((ns, KVH, prompts, XH, HD), bf16),
            pltpu.VMEM((ns, KVH, prompts, XH, HD), bf16),
            pltpu.VMEM((ns, 2, XH, HD), f32),
            pltpu.VMEM((ns, 2, XH, HD), f32),
            pltpu.VMEM((XH, HD), f32),
            dma((KVH,)), dma((KVH,)), dma, dma, dma, dma,
            dma((KVH, 2)), dma((KVH,)), dma((KVH,)), dma((KVH,)), dma((KVH,)),
            dma((KVH,)), dma((KVH,)), dma, dma, dma((KVH,)), dma((4,)),
        ]
        + [pltpu.VMEM((np_, 2, slots, HD), bf16)] * KVH,
        compiler_params=pltpu.CompilerParams(
            collective_id=0, has_side_effects=True, vmem_limit_bytes=60 * 1024 * 1024
        ),
    )(
        owner,
        q,
        pos,
        fresh_keys.reshape(prompts, KVH, HD),
        fresh_values.reshape(prompts, KVH, HD),
        cache_keys.reshape(slots, KVH * HD),
        cache_values.reshape(slots, KVH * HD),
        lens,
    )
    return out.reshape(prompts, 1, H * HD)


def solution(mesh):
    return jax.shard_map(
        on_device,
        mesh=mesh,
        in_specs=(
            P("prompt", "span", None),
            P("prompt", "span"),
            P("prompt", "span", None),
            P("prompt", "span", None),
            P("prompt", "span", None, None),
            P("prompt", "span", None, None),
            P("prompt", "span"),
            P("span", "prompt", None),
        ),
        out_specs=P("prompt", "span", None),
        check_vma=False,
    )
```

time: 245 us -> 74 us (0.30)
  waiting for transfers between devices: 98.5 us -> 0 us
  Pallas kernels: 0 us -> 67.2 us
  matrix products: 30.7 us -> 0 us
  starting transfers between devices: 27.2 us -> 0 us
  local copies, waits for them, and re-layouts: 29.7 us -> 5.85 us
  blocking collectives: 22.4 us -> 0 us
  between operations: 14.3 us -> 0.68 us
  loops' own time: 11.4 us -> 0 us
  other arithmetic: 10 us -> 0 us
    all_to_all x8 -> x0, waiting for transfers between devices: 80.8 us -> none  [the longest x1 24.8 us: on_device(): lax.all_to_all(send_q, 'prompt', split_axis=0, concat_axis=0, tiled=True)]
    pallas_call x0 -> x1, Pallas kernels: none -> 67.2 us  [on_device(): pl.pallas_call(functools.partial(kernel, np_, ns, prompts, slots), out_sh...]
    dot_general x21 -> x0, matrix products: 30.7 us -> none  [the longest x8 13.1 us: per_head(): jnp.dot(weights.astype(jnp.bfloat16).reshape(row_count * group_size, -1),...]
    all_to_all x8 -> x0, starting transfers between devices: 27.2 us -> none  [the longest x1 3.61 us: on_device(): lax.all_to_all(send_q, 'prompt', split_axis=0, concat_axis=0, tiled=True)]
    all_gather x1 -> x0, blocking collectives: 22.4 us -> none  [on_device(): lax.all_gather(query_pos, 'span', axis=1, tiled=True)]
    all_gather x1 -> x0, waiting for transfers between devices: 17 us -> none  [on_device(): lax.all_gather(queries, 'span', axis=1, tiled=True)]
    another operation x1 -> x0, loops' own time: 11.4 us -> none  [attend(): lax.map(per_head, jnp.arange(KVH, dtype=jnp.int32))]
    unnamed x17 -> x4, local copies, waits for them, and re-layouts: 8.2 us -> 0.07 us
  transfers between devices with their start and end apart: 9 -> 0, of which waited for: 7 -> 0; matrix products, arithmetic and copies ran while one was open for 9% -> 0% of each run, Pallas kernels for 0% -> 0%
where the time goes in v1:
time: 74 us; the launch traced here: 73.7 us
  Pallas kernels  67.2 us (91%)
  local copies, waits for them, and re-layouts  5.85 us (8%)
    pallas_call x1, Pallas kernels, on_device(): pl.pallas_call(functools.partial(kernel, np_, ns, prompts, slots), out_sh...  67.2 us
    reshape x1, local copies, waits for them, and re-layouts, on_device(): return out.reshape(prompts, 1, H * HD)  1.62 us
    transpose x1, local copies, waits for them, and re-layouts, on_device(): q = jnp.transpose(queries.reshape(prompts, KVH, XH, HD), (1, 0, 2, 3))  1.58 us

profile of v1, /device:TPU:0, one launch (start us, length us, event | category | flops | bytes accessed | tf_op | source)
XLA Modules:
  0.0 73.7 jit_solution(16797080355142239831)
XLA Ops:
  0.0 0.0 copy-start
  0.7 0.0 copy-start.1
  0.7 0.6 broadcast_in_dim.17.len_ref
  1.3 0.1 copy-done.1
  1.3 0.7 broadcast_in_dim.15.pos_ref
  2.0 0.0 copy-done
  2.0 1.3 %copy_bitcast_fusion.2 = (bf16[8,8,128]{2,1,0:T(8,128)(2,1)}, bf16[8,8,128]{2,1,0:T(8,128)(2,1)}) fusion(bf16[1,8,8,128]{3,1,2,0:T(8,128)(2,1)S(1)} %bitcast.30, bf16[1,8,8,128]{3,1,2,0:T(8,128)(2,1)} %bitcast.31), kind=kLoop, calls=%fused_computation.2 | loop fusion | bytes 65536 | tf_op jit(solution)/shard_map/reshape | solution.py:256
  3.3 1.6 %copy_bitcast_fusion.1.q_ref = bf16[8,8,8,128]{3,2,1,0:T(8,128)(2,1)} fusion(bf16[1,8,64,128]{3,1,2,0:T(8,128)(2,1)} %bitcast.29), kind=kLoop, calls=%fused_computation.1 | loop fusion | bytes 262144 | tf_op jit(solution)/shard_map/transpose | solution.py:221
  4.9 67.2 %shard_map.82 = bf16[8,8,8,128]{3,2,1,0:T(8,128)(2,1)} custom-call(s32[8]{0:T(128)} %bitcast.33, bf16[8,8,8,128]{3,2,1,0:T(8,128)(2,1)} %copy_bitcast_fusion.1.q_ref, s32[8,128]{1,0:T(8,128)} %broadcast_in_dim.15.pos_ref, bf16[8,8,128]{2,1,0:T(8,128)(2,1)} %get-tuple-element.6.fk_ref, bf16[8,8,128]{2,1,0:T(8,128)(2,1)} %get-tuple-element.5.fv_ref, ...), custom_call_target="tpu_custom_call" | custom-call | tf_op jit(solution)/shard_map/pallas_call | solution.py:229
  72.1 1.6 %reshape.27 = bf16[8,1,8192]{2,0,1:T(8,128)(2,1)} reshape(bf16[8,8,8,128]{3,2,1,0:T(8,128)(2,1)} %shard_map.82) | data formatting | bytes 262144 | tf_op jit(solution)/shard_map/reshape | solution.py:261
Async XLA Ops:
  0.0 2.0 %copy-start = (bf16[8,1,1024]{2,0,1:T(8,128)(2,1)S(1)}, bf16[8,1,1024]{2,0,1:T(8,128)(2,1)}, u32[]{:S(2)}) copy-start(bf16[8,1,1024]{2,0,1:T(8,128)(2,1)} %param.11) | copy-start | bytes 49156
  0.7 0.7 copy-start.1

commit v2 on v1

--- a/solution.py
+++ b/solution.py
@@ -19,8 +19,9 @@
 
 def kernel(
     np_, ns, prompts, slots,
-    owner_ref, q_ref, pos_ref, fk_ref, fv_ref, k_ref, v_ref, len_ref,
+    owner_ref, pos_in, len_in, q_in, fk_in, fv_in, k_ref, v_ref,
     out_ref,
+    q_ref, pos_ref, len_ref, fk_ref, fv_ref,
     q_all, pos_all, len_all, part, part_all, stat, stat_all, own_ref,
     q_send, q_recv, pos_send, pos_recv, len_send, len_recv,
     load_sem, kvy_send, kvy_recv, kvp_send, kvp_recv,
@@ -55,8 +56,12 @@
             )
             c.start()
             loads.append(c)
-    q_keep = pltpu.make_async_copy(q_ref, q_all.at[col], own_sem.at[0])
-    q_keep.start()
+    line = lax.broadcasted_iota(jnp.int32, (prompts, HD), 0)
+    pos_tile = jnp.zeros((prompts, HD), jnp.int32)
+    for p in range(prompts):
+        pos_tile = jnp.where(line == p, pos_in[0, p], pos_tile)
+    pos_ref[...] = pos_tile
+    len_ref[...] = jnp.full((XH, HD), len_in[0, 0], jnp.int32)
     pos_keep = pltpu.make_async_copy(pos_ref, pos_all.at[col], own_sem.at[1])
     pos_keep.start()
     len_keep = pltpu.make_async_copy(len_ref, len_all.at[row], own_sem.at[2])
@@ -79,19 +84,32 @@
         for r in y_peers:
             send(kv[g].at[row], kv[g].at[row], kvy_send.at[g], kvy_recv.at[g], r, col)
         send(kv[g].at[row], kv[g].at[row], kvp_send.at[g], kvp_recv.at[g], partner, col)
+
+    for g in range(KVH):
+        tiles = [
+            q_in[:, (g * XH + x) * HD : (g * XH + x + 1) * HD].astype(jnp.float32)
+            for x in range(XH)
+        ]
+        q_ref[g] = jnp.swapaxes(jnp.stack(tiles, axis=0), 0, 1).astype(jnp.bfloat16)
         for s in span_peers:
             send(q_ref.at[g], q_all.at[col, g], q_send.at[g], q_recv.at[g], row, s)
+
+    q_keep = pltpu.make_async_copy(q_ref, q_all.at[col], own_sem.at[0])
+    q_keep.start()
+    for g in range(KVH):
+        cols = slice(g * HD, (g + 1) * HD)
+        fk_ref[g] = fk_in[:, cols].astype(jnp.float32)
+        fv_ref[g] = fv_in[:, cols].astype(jnp.float32)
 
     lane = lax.broadcasted_iota(jnp.int32, (XH, HD), 1)
     own_ref[...] = jnp.zeros_like(own_ref)
     stat[...] = jnp.zeros_like(stat)
 
     def own_body(p, carry):
-        keys = fk_ref[p].astype(jnp.float32)
         tile = own_ref[...]
         for g in range(KVH):
             q8 = q_ref[g, p].astype(jnp.float32)
-            dot = jnp.sum(q8 * keys[g : g + 1], axis=1, keepdims=True)
+            dot = jnp.sum(q8 * fk_ref[g, pl.ds(p, 1), :], axis=1, keepdims=True)
             tile = jnp.where(lane == g * prompts + p, dot * (1.0 / math.sqrt(HD)), tile)
         own_ref[...] = tile
         return carry
@@ -111,15 +129,15 @@
     step = 2 if prompts % 2 == 0 else 1
 
     for g in range(KVH):
-        wait_bytes(q_all.at[pl.ds(0, ns - 1), g], q_recv.at[g])
         if rows_y > 1:
             wait_bytes(kv[g].at[pl.ds(0, rows_y - 1)], kvy_recv.at[g])
         for r in y_peers:
             send(kv[g].at[r], kv[g].at[r], kvp_send.at[g], kvp_recv.at[g], partner, col)
+        wait_bytes(q_all.at[pl.ds(0, ns - 1), g], q_recv.at[g])
         wait_bytes(kv[g].at[pl.ds(0, rows_y)], kvp_recv.at[g])
 
         def one(p, g=g):
-            o = owner_ref[p]
+            o = owner_ref[0, p]
             q64 = q_all[:, g, p].astype(jnp.float32).reshape(count, HD).astype(jnp.bfloat16)
             keys = kv[g][o, 0]
             values = kv[g][o, 1]
@@ -184,11 +202,10 @@
     def combine(p, carry):
         shift = lax.rem(HD - p, HD)
         own_s = pltpu.roll(own_ref[...], shift, 1)
-        fresh = fv_ref[p].astype(jnp.float32)
         sums = []
         for g in range(KVH):
             lo = g * prompts
-            sums.append(own_s[:, lo : lo + 1] * fresh[g : g + 1])
+            sums.append(own_s[:, lo : lo + 1] * fv_ref[g, pl.ds(p, 1), :])
         for j in range(ns):
             f = pltpu.roll(stat_all[j, 0], shift, 1)
             for g in range(KVH):
@@ -218,10 +235,6 @@
     slots = cache_keys.shape[2]
     np_ = lax.axis_size("prompt")
     ns = lax.axis_size("span")
-    q = jnp.transpose(queries.reshape(prompts, KVH, XH, HD), (1, 0, 2, 3))
-    pos = jnp.broadcast_to(query_pos.reshape(prompts, 1), (prompts, HD))
-    lens = jnp.broadcast_to(block_len.reshape(1, 1), (XH, HD))
-    owner = block_owner.reshape(prompts)
     vmem = pl.BlockSpec(memory_space=pltpu.VMEM)
     hbm = pl.BlockSpec(memory_space=pl.ANY)
     dma = pltpu.SemaphoreType.DMA
@@ -229,9 +242,14 @@
     out = pl.pallas_call(
         functools.partial(kernel, np_, ns, prompts, slots),
         out_shape=jax.ShapeDtypeStruct((prompts, KVH, XH, HD), bf16),
-        in_specs=[pl.BlockSpec(memory_space=pltpu.SMEM)] + [vmem] * 4 + [hbm] * 2 + [vmem],
+        in_specs=[pl.BlockSpec(memory_space=pltpu.SMEM)] * 3 + [vmem] * 3 + [hbm] * 2,
         out_specs=vmem,
         scratch_shapes=[
+            pltpu.VMEM((KVH, prompts, XH, HD), bf16),
+            pltpu.VMEM((prompts, HD), i32),
+            pltpu.VMEM((XH, HD), i32),
+            pltpu.VMEM((KVH, prompts, HD), f32),
+            pltpu.VMEM((KVH, prompts, HD), f32),
             pltpu.VMEM((ns, KVH, prompts, XH, HD), bf16),
             pltpu.VMEM((ns, prompts, HD), i32),
             pltpu.VMEM((np_, XH, HD), i32),
@@ -249,14 +267,14 @@
             collective_id=0, has_side_effects=True, vmem_limit_bytes=60 * 1024 * 1024
         ),
     )(
-        owner,
-        q,
-        pos,
-        fresh_keys.reshape(prompts, KVH, HD),
-        fresh_values.reshape(prompts, KVH, HD),
+        block_owner.reshape(1, prompts),
+        query_pos.reshape(1, prompts),
+        block_len,
+        queries.reshape(prompts, H * HD),
+        fresh_keys.reshape(prompts, KVH * HD),
+        fresh_values.reshape(prompts, KVH * HD),
         cache_keys.reshape(slots, KVH * HD),
         cache_values.reshape(slots, KVH * HD),
-        lens,
     )
     return out.reshape(prompts, 1, H * HD)
 

time: 74 us -> 69.5 us (0.939)
  local copies, waits for them, and re-layouts: 5.85 us -> 1.62 us
    transpose x1 -> x0, local copies, waits for them, and re-layouts: 1.58 us -> none  [on_device(): q = jnp.transpose(queries.reshape(prompts, KVH, XH, HD), (1, 0, 2, 3))]
    reshape x1 -> x0, local copies, waits for them, and re-layouts: 1.34 us -> none  [on_device(): fresh_values.reshape(prompts, KVH, HD)]
    broadcast_in_dim x2 -> x0, local copies, waits for them, and re-layouts: 1.24 us -> none  [the longest x1 0.65 us: on_device(): pos = jnp.broadcast_to(query_pos.reshape(prompts, 1), (prompts, HD))]
where the time goes in v2:
time: 69.5 us; the launch traced here: 69.3 us
  Pallas kernels  67 us (96%)
  local copies, waits for them, and re-layouts  1.62 us (2%)
    pallas_call x1, Pallas kernels, on_device(): pl.pallas_call(functools.partial(kernel, np_, ns, prompts, slots), out_sh...  67 us
    reshape x1, local copies, waits for them, and re-layouts, on_device(): return out.reshape(prompts, 1, H * HD)  1.62 us

profile of v2, /device:TPU:0, one launch (start us, length us, event | category | flops | bytes accessed | tf_op | source)
XLA Modules:
  0.0 69.3 jit_solution(18445078958840850595)
XLA Ops:
  0.7 67.0 %shard_map.82 = bf16[8,8,8,128]{3,2,1,0:T(8,128)(2,1)} custom-call(s32[1,8]{1,0:T(1,128)} %bitcast.14, s32[1,8]{1,0:T(1,128)} %bitcast.15, s32[1,1]{1,0:T(1,128)S(6)} %copy.9.len_in, bf16[8,8192]{1,0:T(8,128)(2,1)} %bitcast.11, bf16[8,1024]{1,0:T(8,128)(2,1)} %bitcast.12, bf16[8,1024]{1,0:T(8,128)(2,1)} %bitcast.13, bf16[512,1024]{1,0:T(8,128)(2,1)} %bitcast.9, ...), custom_call_target="tpu_custom_call" | custom-call | tf_op jit(solution)/shard_map/pallas_call | solution.py:242
  67.7 1.6 %reshape.31 = bf16[8,1,8192]{2,0,1:T(8,128)(2,1)} reshape(bf16[8,8,8,128]{3,2,1,0:T(8,128)(2,1)} %shard_map.82) | data formatting | bytes 262144 | tf_op jit(solution)/shard_map/reshape | solution.py:279
